TPU v7x, 512 devices: a whole 4x8x8 slice. The times are simulated.
512 devices in a mesh: sub: 16 (over z, core), blk: 32 (over x, y).
Axes of the slice: x: 4, y: 8, z: 8, core: 2. Of those that a mesh axis runs over, the one named last changes fastest.
Arguments:
- double_layer: bfloat16 [16, 2, 2048, 2048], P('sub', None, 'blk'), may hold values from -1 to 2
- single_layer: bfloat16 [16, 2, 2048, 2048], P('sub', None, 'blk'), may hold values from -1 to 2
- hypersingular: bfloat16 [16, 2, 2048, 2048], P('sub', None, 'blk'), may hold values from -1 to 2
- adjoint_double: bfloat16 [16, 2, 2048, 2048], P('sub', None, 'blk'), may hold values from -1 to 2
- matching: int32 [16, 1024], replicated, may hold values from 0 to 1023, each once within a row
- right_side: float32 [16, 2, 2, 2048, 64], P('sub', None, None, 'blk'), may hold values from -6 to 6
- start: float32 [16, 2, 2, 2048, 64], P('sub', None, None, 'blk'), may hold values from -4 to 4
Outputs:
- solution: float32 [16, 2, 2, 2048, 64], P('sub', None, None, 'blk')
Inputs may be any that keep to these rules, and one draw needn't show every extreme that they name: `matching`: each row is a permutation of 0 to 1023; row 0 pairs with no subdomain below and is not read.
All inputs are finite; a program needn't handle non-finite values.
Results may differ from a plain program's by a relative error of at most 0.015.
Values may be sent and summed in bfloat16 or wider, within the bound.
No kernel may reach another device: no remote copies, remote signals or barrier semaphores. Data moves between devices by JAX's collectives and lax.ppermute only.
A program may use at most 64 MiB of HBM per device.

v0:
```python
import jax
import jax.numpy as jnp
from jax import lax
from jax.sharding import Mesh
from jax.sharding import PartitionSpec as P

BASIS = 5
SUB = ("sub_0", "sub_1")
BLK = ("blk_0", "blk_1")
SUB_BLK = ("sub_0", "sub_1", "blk_0", "blk_1")
EPSILON = 1e-06


def passed_along(block, axis, distance):
    devices = range(lax.axis_size(axis))
    route = [(i - distance, i) for i in devices if i - distance in devices]
    return lax.ppermute(block, axis, route)


def copy_for_each(value, axis):
    peers = lax.axis_size(axis)
    return lax.all_to_all(
        jnp.broadcast_to(value[None], (peers, *value.shape)), axis, 0, 0, tiled=True
    )


def laid_out(blocks, dim):
    blocks = jnp.moveaxis(blocks, 0, dim)
    lengths = blocks.shape
    return blocks.reshape(*lengths[:dim], lengths[dim] * lengths[dim + 1], *lengths[dim + 2 :])


def gathered_copies(value, axis, dim):
    blocks = copy_for_each(value, axis)
    return laid_out(blocks, dim)


def over_axes(value, axes):
    for axis in axes:
        value = lax.psum(value, axis)
    return value


def complex_product(matrix, vector):
    width = vector.shape[-1] // 2
    count = matrix.shape[1]
    products = jnp.dot(
        matrix.reshape(2 * count, matrix.shape[2]), vector, preferred_element_type=jnp.float32
    )
    products = products.reshape(2, count, 2 * width)
    real_part = products[0, :, :width] - products[1, :, width:]
    imag_part = products[0, :, width:] + products[1, :, :width]
    return jnp.concatenate([real_part, imag_part], axis=-1)


def calderon(double_layer, single_layer, hypersingular, adjoint_double, vector):
    upper = complex_product(single_layer, vector[1]) - complex_product(double_layer, vector[0])
    lower = complex_product(hypersingular, vector[0]) + complex_product(adjoint_double, vector[1])
    return jnp.stack([upper, lower])


def inward(field):
    local_field = field[0]
    return jnp.concatenate([local_field[:, 0], local_field[:, 1]], axis=-1)


def outward(vector):
    width = vector.shape[-1] // 2
    return jnp.stack([vector[..., :width], vector[..., width:]], axis=1)[None]


def coupling_rows(gathered, matching, local_rows):
    subdomains = lax.axis_size(SUB)
    own_index = lax.axis_index(SUB)
    block_index = lax.axis_index(BLK)
    half_rows = local_rows // 2
    above_index = jnp.minimum(own_index + 1, subdomains - 1)
    perm_here = lax.dynamic_index_in_dim(matching, own_index, 0, keepdims=False)
    perm_above = lax.dynamic_index_in_dim(matching, above_index, 0, keepdims=False)
    window = block_index * half_rows
    odd_rows = gathered[:, 1::2]
    even_rows = gathered[:, 0::2]
    inverse_here = jnp.argsort(perm_here)
    send_upward = jnp.take(
        odd_rows, lax.dynamic_slice_in_dim(perm_above, window, half_rows), axis=1
    )
    send_downward = jnp.take(
        even_rows, lax.dynamic_slice_in_dim(inverse_here, window, half_rows), axis=1
    )
    lower_face = passed_along(send_upward, SUB, 1)
    upper_face = passed_along(send_downward, SUB, -1)
    joined = jnp.stack([lower_face, upper_face], axis=2)
    joined = joined.reshape(2, local_rows, gathered.shape[-1]).astype(jnp.float32)
    trace_signs = jnp.array([1.0, -1.0], jnp.float32).reshape(2, 1, 1)
    return joined * trace_signs


def preconditioned(operators, matching, vector):
    rounded = vector.astype(jnp.bfloat16)
    gathered = gathered_copies(rounded, BLK, 1)
    first_image = calderon(*operators, gathered)
    middle = first_image - 0.5 * coupling_rows(gathered, matching, vector.shape[1])
    middle_rounded = middle.astype(jnp.bfloat16)
    middle_full = gathered_copies(middle_rounded, BLK, 1)
    return calderon(*operators, middle_full)


def inner_local(first, second):
    totals = jnp.sum(first * second, axis=(0, 1))
    width = totals.shape[0] // 2
    return totals[:width] + totals[width:]


def spread(values):
    return jnp.concatenate([values, values])


def global_norm(vector):
    return jnp.sqrt(over_axes(inner_local(vector, vector), SUB_BLK) + EPSILON)


def body(double_layer, single_layer, hypersingular, adjoint_double, matching, right_side, start):
    operators = (double_layer[0], single_layer[0], hypersingular[0], adjoint_double[0])
    right_local = inward(right_side)
    start_local = inward(start)
    residual = right_local - preconditioned(operators, matching, start_local)
    beta = global_norm(residual)
    basis = [residual / spread(beta)]
    columns = []
    for column in range(BASIS):
        image = preconditioned(operators, matching, basis[column])
        local_dots = [inner_local(basis[earlier], image) for earlier in range(column + 1)]
        stacked_dots = jnp.stack(local_dots + [inner_local(image, image)])
        summed = over_axes(stacked_dots, SUB_BLK)
        coefficients = [summed[earlier] for earlier in range(column + 1)]
        for earlier in range(column + 1):
            image = image - spread(coefficients[earlier]) * basis[earlier]
        squares = summed[column + 1] - jnp.sum(summed[: column + 1] * summed[: column + 1], axis=0)
        height = jnp.sqrt(jnp.maximum(squares, 0.0) + EPSILON)
        if column + 1 < BASIS:
            basis.append(image / spread(height))
        filler = [jnp.zeros_like(height)] * (BASIS - 1 - column)
        columns.append(jnp.stack(coefficients + [height] + filler, axis=1))
    hessen = jnp.stack(columns, axis=2)
    gram = jnp.einsum("rij,rik->rjk", hessen, hessen, precision=lax.Precision.HIGHEST)
    target = beta[:, None] * hessen[:, 0, :]
    factor = jnp.linalg.cholesky(gram)
    weights = jax.scipy.linalg.cho_solve((factor, True), target[..., None])[..., 0]
    solution = start_local
    for column in range(BASIS):
        solution = solution + spread(weights[:, column]) * basis[column]
    return outward(solution)


def solution(mesh):
    torus = Mesh(mesh.devices.reshape(8, 2, 4, 8), ("sub_0", "sub_1", "blk_0", "blk_1"))
    placed = (
        P(SUB, None, BLK, None),
        P(SUB, None, BLK, None),
        P(SUB, None, BLK, None),
        P(SUB, None, BLK, None),
        P(),
        P(SUB, None, None, BLK, None),
        P(SUB, None, None, BLK, None),
    )
    return jax.shard_map(
        body, mesh=torus, in_specs=placed, out_specs=P(SUB, None, None, BLK, None), check_vma=False
    )
```

profile of v0, /device:TPU:2, one launch (start us, length us, event | category | flops | bytes accessed | tf_op | source)
XLA Modules:
  0.0 825.8 jit_solution(2891582693578804265)
XLA Ops:
  2.9 10.3 %all-to-all-start = ((bf16[32,2,64,128]{3,2,1,0:T(8,128)(2,1)}), bf16[32,2,64,128]{3,2,1,0:T(8,128)(2,1)S(1)}, u32[]{:S(2)}, u32[]{:S(2)}) async-start(bf16[32,2,64,128]{3,2,1,0:T(8,128)(2,1)} %broadcast_in_dim.37), calls=%async_computation | async-start | bytes 2097152 | tf_op jit(solution)/shard_map/all_to_all | solution.py:22
  19.2 20.1 %all-to-all-done = bf16[32,2,64,128]{3,2,1,0:T(8,128)(2,1)S(1)} async-done(((bf16[32,2,64,128]{3,2,1,0:T(8,128)(2,1)}), bf16[32,2,64,128]{3,2,1,0:T(8,128)(2,1)S(1)}, u32[]{:S(2)}, u32[]{:S(2)}) %all-to-all-start) | async-done | bytes 1048608 | tf_op jit(solution)/shard_map/all_to_all | solution.py:22
  61.9 24.3 %all-to-all-done.1 = bf16[32,2,64,128]{3,2,1,0:T(8,128)(2,1)S(1)} async-done(((bf16[32,2,64,128]{3,2,1,0:T(8,128)(2,1)}), bf16[32,2,64,128]{3,2,1,0:T(8,128)(2,1)S(1)}, u32[]{:S(2)}, u32[]{:S(2)}) %all-to-all-start.1) | async-done | bytes 1048608 | tf_op jit(solution)/shard_map/all_to_all | solution.py:22
  88.2 26.7 %psum.168 = f32[64]{0:T(128)S(1)} all-reduce(f32[64]{0:T(128)S(1)} %slice_add_fusion.48), channel_id=1, replica_groups=mesh['sub_0'=8,'sub_1'=2,'blk_0'=4,'blk_1'=8] {'sub_0'}, use_global_device_ids=true, to_apply=%region_2.4 | all-reduce | flops 64 | bytes 512 | tf_op jit(solution)/shard_map/psum | solution.py:40
  117.3 10.5 %psum.170 = f32[64]{0:T(128)S(1)} all-reduce(f32[64]{0:T(128)S(1)} %psum.169), channel_id=1, replica_groups=mesh['sub_0'=8,'sub_1'=2,'blk_0'=4,'blk_1'=8] {'blk_0'}, use_global_device_ids=true, to_apply=%region_4.6 | all-reduce | flops 64 | bytes 512 | tf_op jit(solution)/shard_map/psum | solution.py:40
  127.8 15.8 %psum.171 = f32[64]{0:T(128)S(1)} all-reduce(f32[64]{0:T(128)S(1)} %psum.170), channel_id=1, replica_groups=mesh['sub_0'=8,'sub_1'=2,'blk_0'=4,'blk_1'=8] {'blk_1'}, use_global_device_ids=true, to_apply=%region_5.7 | all-reduce | flops 64 | bytes 512 | tf_op jit(solution)/shard_map/psum | solution.py:40
  144.5 26.8 %all_to_all.60 = bf16[32,2,64,128]{3,2,1,0:T(8,128)(2,1)S(1)} all-to-all(bf16[32,2,64,128]{3,2,1,0:T(8,128)(2,1)S(1)} %broadcast_in_dim.39), channel_id=1, replica_groups=mesh['sub_0'=8,'sub_1'=2,'blk_0'=4,'blk_1'=8] {'blk_0','blk_1'}, dimensions={0} | all-to-all | bytes 2097152 | tf_op jit(solution)/shard_map/all_to_all | solution.py:22
  188.8 34.5 %all_to_all.61 = bf16[32,2,64,128]{3,2,1,0:T(8,128)(2,1)S(1)} all-to-all(bf16[32,2,64,128]{3,2,1,0:T(8,128)(2,1)S(1)} %broadcast_in_dim.40), channel_id=1, replica_groups=mesh['sub_0'=8,'sub_1'=2,'blk_0'=4,'blk_1'=8] {'blk_0','blk_1'}, dimensions={0} | all-to-all | bytes 2097152 | tf_op jit(solution)/shard_map/all_to_all | solution.py:22
  225.2 14.5 %psum.172 = f32[2,64]{1,0:T(2,128)S(1)} all-reduce(f32[2,64]{1,0:T(2,128)S(1)} %pad_maximum_fusion.8), channel_id=1, replica_groups=mesh['sub_0'=8,'sub_1'=2,'blk_0'=4,'blk_1'=8] {'sub_0'}, use_global_device_ids=true, to_apply=%region_8.10 | all-reduce | flops 128 | bytes 1024 | tf_op jit(solution)/shard_map/psum | solution.py:40
  242.2 10.4 %psum.174 = f32[2,64]{1,0:T(2,128)S(1)} all-reduce(f32[2,64]{1,0:T(2,128)S(1)} %psum.173), channel_id=1, replica_groups=mesh['sub_0'=8,'sub_1'=2,'blk_0'=4,'blk_1'=8] {'blk_0'}, use_global_device_ids=true, to_apply=%region_10.12 | all-reduce | flops 128 | bytes 1024 | tf_op jit(solution)/shard_map/psum | solution.py:40
  252.6 15.9 %psum.175 = f32[2,64]{1,0:T(2,128)S(1)} all-reduce(f32[2,64]{1,0:T(2,128)S(1)} %psum.174), channel_id=1, replica_groups=mesh['sub_0'=8,'sub_1'=2,'blk_0'=4,'blk_1'=8] {'blk_1'}, use_global_device_ids=true, to_apply=%region_11.13 | all-reduce | flops 128 | bytes 1024 | tf_op jit(solution)/shard_map/psum | solution.py:40
  270.0 26.8 %all_to_all.62 = bf16[32,2,64,128]{3,2,1,0:T(8,128)(2,1)S(1)} all-to-all(bf16[32,2,64,128]{3,2,1,0:T(8,128)(2,1)S(1)} %broadcast_in_dim.41), channel_id=1, replica_groups=mesh['sub_0'=8,'sub_1'=2,'blk_0'=4,'blk_1'=8] {'blk_0','blk_1'}, dimensions={0} | all-to-all | bytes 2097152 | tf_op jit(solution)/shard_map/all_to_all | solution.py:22
  316.5 34.5 %all_to_all.63 = bf16[32,2,64,128]{3,2,1,0:T(8,128)(2,1)S(1)} all-to-all(bf16[32,2,64,128]{3,2,1,0:T(8,128)(2,1)S(1)} %broadcast_in_dim.42), channel_id=1, replica_groups=mesh['sub_0'=8,'sub_1'=2,'blk_0'=4,'blk_1'=8] {'blk_0','blk_1'}, dimensions={0} | all-to-all | bytes 2097152 | tf_op jit(solution)/shard_map/all_to_all | solution.py:22
  353.1 15.5 %psum.176 = f32[3,64]{1,0:T(4,128)S(1)} all-reduce(f32[3,64]{1,0:T(4,128)S(1)} %pad_maximum_fusion.6), channel_id=1, replica_groups=mesh['sub_0'=8,'sub_1'=2,'blk_0'=4,'blk_1'=8] {'sub_0'}, use_global_device_ids=true, to_apply=%region_15.17 | all-reduce | flops 192 | bytes 1536 | tf_op jit(solution)/shard_map/psum | solution.py:40
  371.0 10.1 %psum.178 = f32[3,64]{1,0:T(4,128)S(1)} all-reduce(f32[3,64]{1,0:T(4,128)S(1)} %psum.177), channel_id=1, replica_groups=mesh['sub_0'=8,'sub_1'=2,'blk_0'=4,'blk_1'=8] {'blk_0'}, use_global_device_ids=true, to_apply=%region_17.19 | all-reduce | flops 192 | bytes 1536 | tf_op jit(solution)/shard_map/psum | solution.py:40
  381.1 16.3 %psum.179 = f32[3,64]{1,0:T(4,128)S(1)} all-reduce(f32[3,64]{1,0:T(4,128)S(1)} %psum.178), channel_id=1, replica_groups=mesh['sub_0'=8,'sub_1'=2,'blk_0'=4,'blk_1'=8] {'blk_1'}, use_global_device_ids=true, to_apply=%region_18.20 | all-reduce | flops 192 | bytes 1536 | tf_op jit(solution)/shard_map/psum | solution.py:40
  399.0 27.0 %all_to_all.64 = bf16[32,2,64,128]{3,2,1,0:T(8,128)(2,1)S(1)} all-to-all(bf16[32,2,64,128]{3,2,1,0:T(8,128)(2,1)S(1)} %broadcast_in_dim.43), channel_id=1, replica_groups=mesh['sub_0'=8,'sub_1'=2,'blk_0'=4,'blk_1'=8] {'blk_0','blk_1'}, dimensions={0} | all-to-all | bytes 2097152 | tf_op jit(solution)/shard_map/all_to_all | solution.py:22
  446.8 33.8 %all_to_all.65 = bf16[32,2,64,128]{3,2,1,0:T(8,128)(2,1)S(1)} all-to-all(bf16[32,2,64,128]{3,2,1,0:T(8,128)(2,1)S(1)} %broadcast_in_dim.44), channel_id=1, replica_groups=mesh['sub_0'=8,'sub_1'=2,'blk_0'=4,'blk_1'=8] {'blk_0','blk_1'}, dimensions={0} | all-to-all | bytes 2097152 | tf_op jit(solution)/shard_map/all_to_all | solution.py:22
  482.7 15.8 %psum.180 = f32[4,64]{1,0:T(4,128)S(1)} all-reduce(f32[4,64]{1,0:T(4,128)S(1)} %pad_maximum_fusion.7), channel_id=1, replica_groups=mesh['sub_0'=8,'sub_1'=2,'blk_0'=4,'blk_1'=8] {'sub_0'}, use_global_device_ids=true, to_apply=%region_24.26 | all-reduce | flops 256 | bytes 2048 | tf_op jit(solution)/shard_map/psum | solution.py:40
  501.0 10.5 %psum.182 = f32[4,64]{1,0:T(4,128)S(1)} all-reduce(f32[4,64]{1,0:T(4,128)S(1)} %psum.181), channel_id=1, replica_groups=mesh['sub_0'=8,'sub_1'=2,'blk_0'=4,'blk_1'=8] {'blk_0'}, use_global_device_ids=true, to_apply=%region_26.28 | all-reduce | flops 256 | bytes 2048 | tf_op jit(solution)/shard_map/psum | solution.py:40
  511.5 15.8 %psum.183 = f32[4,64]{1,0:T(4,128)S(1)} all-reduce(f32[4,64]{1,0:T(4,128)S(1)} %psum.182), channel_id=1, replica_groups=mesh['sub_0'=8,'sub_1'=2,'blk_0'=4,'blk_1'=8] {'blk_1'}, use_global_device_ids=true, to_apply=%region_27.29 | all-reduce | flops 256 | bytes 2048 | tf_op jit(solution)/shard_map/psum | solution.py:40
  528.8 26.8 %all_to_all.66 = bf16[32,2,64,128]{3,2,1,0:T(8,128)(2,1)S(1)} all-to-all(bf16[32,2,64,128]{3,2,1,0:T(8,128)(2,1)S(1)} %broadcast_in_dim.45), channel_id=1, replica_groups=mesh['sub_0'=8,'sub_1'=2,'blk_0'=4,'blk_1'=8] {'blk_0','blk_1'}, dimensions={0} | all-to-all | bytes 2097152 | tf_op jit(solution)/shard_map/all_to_all | solution.py:22
  577.8 33.7 %all_to_all.67 = bf16[32,2,64,128]{3,2,1,0:T(8,128)(2,1)S(1)} all-to-all(bf16[32,2,64,128]{3,2,1,0:T(8,128)(2,1)S(1)} %broadcast_in_dim.46), channel_id=1, replica_groups=mesh['sub_0'=8,'sub_1'=2,'blk_0'=4,'blk_1'=8] {'blk_0','blk_1'}, dimensions={0} | all-to-all | bytes 2097152 | tf_op jit(solution)/shard_map/all_to_all | solution.py:22
  613.8 15.9 %psum.184 = f32[5,64]{1,0:T(8,128)S(1)} all-reduce(f32[5,64]{1,0:T(8,128)S(1)} %stack.288), channel_id=1, replica_groups=mesh['sub_0'=8,'sub_1'=2,'blk_0'=4,'blk_1'=8] {'sub_0'}, use_global_device_ids=true, to_apply=%region_34.36 | all-reduce | flops 320 | bytes 2560 | tf_op jit(solution)/shard_map/psum | solution.py:40
  632.1 10.4 %psum.186 = f32[5,64]{1,0:T(8,128)S(1)} all-reduce(f32[5,64]{1,0:T(8,128)S(1)} %psum.185), channel_id=1, replica_groups=mesh['sub_0'=8,'sub_1'=2,'blk_0'=4,'blk_1'=8] {'blk_0'}, use_global_device_ids=true, to_apply=%region_36.38 | all-reduce | flops 320 | bytes 2560 | tf_op jit(solution)/shard_map/psum | solution.py:40
  642.6 15.7 %psum.187 = f32[5,64]{1,0:T(8,128)S(1)} all-reduce(f32[5,64]{1,0:T(8,128)S(1)} %psum.186), channel_id=1, replica_groups=mesh['sub_0'=8,'sub_1'=2,'blk_0'=4,'blk_1'=8] {'blk_1'}, use_global_device_ids=true, to_apply=%region_37.39 | all-reduce | flops 320 | bytes 2560 | tf_op jit(solution)/shard_map/psum | solution.py:40
  660.4 27.0 %all_to_all.68 = bf16[32,2,64,128]{3,2,1,0:T(8,128)(2,1)S(1)} all-to-all(bf16[32,2,64,128]{3,2,1,0:T(8,128)(2,1)S(1)} %broadcast_in_dim.47), channel_id=1, replica_groups=mesh['sub_0'=8,'sub_1'=2,'blk_0'=4,'blk_1'=8] {'blk_0','blk_1'}, dimensions={0} | all-to-all | bytes 2097152 | tf_op jit(solution)/shard_map/all_to_all | solution.py:22
  725.5 19.4 %all-to-all-done.11 = bf16[32,2,64,128]{3,2,1,0:T(8,128)(2,1)S(1)} async-done(((bf16[32,2,64,128]{3,2,1,0:T(8,128)(2,1)}), bf16[32,2,64,128]{3,2,1,0:T(8,128)(2,1)S(1)}, u32[]{:S(2)}, u32[]{:S(2)}) %all-to-all-start.11) | async-done | bytes 1048608 | tf_op jit(solution)/shard_map/all_to_all | solution.py:22
  747.9 15.7 %psum.188 = f32[6,64]{1,0:T(8,128)S(1)} all-reduce(f32[6,64]{1,0:T(8,128)S(1)} %stack.302), channel_id=1, replica_groups=mesh['sub_0'=8,'sub_1'=2,'blk_0'=4,'blk_1'=8] {'sub_0'}, use_global_device_ids=true, to_apply=%region_45.47 | all-reduce | flops 384 | bytes 3072 | tf_op jit(solution)/shard_map/psum | solution.py:40
  766.1 10.4 %psum.190 = f32[6,64]{1,0:T(8,128)S(1)} all-reduce(f32[6,64]{1,0:T(8,128)S(1)} %psum.189), channel_id=1, replica_groups=mesh['sub_0'=8,'sub_1'=2,'blk_0'=4,'blk_1'=8] {'blk_0'}, use_global_device_ids=true, to_apply=%region_47.49 | all-reduce | flops 384 | bytes 3072 | tf_op jit(solution)/shard_map/psum | solution.py:40
  776.5 15.7 %psum.191 = f32[6,64]{1,0:T(8,128)S(1)} all-reduce(f32[6,64]{1,0:T(8,128)S(1)} %psum.190), channel_id=1, replica_groups=mesh['sub_0'=8,'sub_1'=2,'blk_0'=4,'blk_1'=8] {'blk_1'}, use_global_device_ids=true, to_apply=%region_48.50 | all-reduce | flops 384 | bytes 3072 | tf_op jit(solution)/shard_map/psum | solution.py:40
  794.2 29.4 %custom-call.11 = f32[64,5,5]{2,1,0:T(8,128)S(1)} custom-call(f32[64,5,5]{2,1,0:T(8,128)S(1)} %fusion), custom_call_target="Cholesky" | custom-call | tf_op jit(solution)/shard_map/jit(cholesky)/cholesky | solution.py:147
  (497 shorter events, 187.5 us)
Async XLA Ops:
  0.0 50.0 %copy-start = (bf16[1,2,64,2048]{3,2,1,0:T(8,128)(2,1)S(1)}, bf16[1,2,64,2048]{3,2,1,0:T(8,128)(2,1)}, u32[]{:S(2)}) copy-start(bf16[1,2,64,2048]{3,2,1,0:T(8,128)(2,1)} %param.16) | copy-start | bytes 1572868
  2.9 36.4 %all-to-all-start = ((bf16[32,2,64,128]{3,2,1,0:T(8,128)(2,1)}), bf16[32,2,64,128]{3,2,1,0:T(8,128)(2,1)S(1)}, u32[]{:S(2)}, u32[]{:S(2)}) async-start(bf16[32,2,64,128]{3,2,1,0:T(8,128)(2,1)} %broadcast_in_dim.37), calls=%async_computation | async-start | bytes 2097152 | tf_op jit(solution)/shard_map/all_to_all | solution.py:22
  18.4 163.4 %copy-start.30 = (pred[32]{0:T(512)(128)(4,1)}, pred[32]{0:T(512)(128)(4,1)S(1)}, u32[]{:S(2)}) copy-start(pred[32]{0:T(512)(128)(4,1)S(1)} %get-tuple-element.40) | copy-start | bytes 100
  19.2 165.2 %copy-start.25 = (pred[32]{0:T(512)(128)(4,1)}, pred[32]{0:T(512)(128)(4,1)S(1)}, u32[]{:S(2)}) copy-start(pred[32]{0:T(512)(128)(4,1)S(1)} %get-tuple-element.38) | copy-start | bytes 100
  19.2 162.0 %copy-start.39 = (s32[1024]{0:T(1024)}, s32[1024]{0:T(1024)S(1)}, u32[]{:S(2)}) copy-start(s32[1024]{0:T(1024)S(1)} %get-tuple-element.215) | copy-start | bytes 12292
  19.2 164.6 %copy-start.38 = (s32[1024]{0:T(1024)}, s32[1024]{0:T(1024)S(1)}, u32[]{:S(2)}) copy-start(s32[1024]{0:T(1024)S(1)} %get-tuple-element.216) | copy-start | bytes 12292
  43.7 8.0 collective-permute-start
  46.3 5.7 collective-permute-start.1
  54.0 7.8 copy-start.24
  54.1 32.1 %all-to-all-start.1 = ((bf16[32,2,64,128]{3,2,1,0:T(8,128)(2,1)}), bf16[32,2,64,128]{3,2,1,0:T(8,128)(2,1)S(1)}, u32[]{:S(2)}, u32[]{:S(2)}) async-start(bf16[32,2,64,128]{3,2,1,0:T(8,128)(2,1)} %broadcast_in_dim.38), calls=%async_computation.1 | async-start | bytes 2097152 | tf_op jit(solution)/shard_map/all_to_all | solution.py:22
  180.7 2.6 copy-start.5
  181.9 6.2 collective-permute-start.3
  184.5 3.9 collective-permute-start.2
  306.2 3.9 copy-start.6
  308.9 6.3 collective-permute-start.5
  311.6 3.9 collective-permute-start.4
  435.9 3.9 copy-start.7
  438.6 6.4 collective-permute-start.7
  439.9 1.4 copy-start.27
  440.4 4.0 copy-start.17
  441.4 4.3 collective-permute-start.6
  566.2 3.9 copy-start.8
  568.8 7.2 collective-permute-start.9
  570.1 1.4 copy-start.28
  570.7 4.0 copy-start.18
  571.7 5.1 collective-permute-start.8
  698.1 3.9 copy-start.4
  700.7 7.4 collective-permute-start.11
  702.5 4.2 copy-start.16
  703.5 5.3 collective-permute-start.10
  710.9 34.0 %all-to-all-start.11 = ((bf16[32,2,64,128]{3,2,1,0:T(8,128)(2,1)}), bf16[32,2,64,128]{3,2,1,0:T(8,128)(2,1)S(1)}, u32[]{:S(2)}, u32[]{:S(2)}) async-start(bf16[32,2,64,128]{3,2,1,0:T(8,128)(2,1)} %broadcast_in_dim.48), calls=%async_computation.11 | async-start | bytes 2097152 | tf_op jit(solution)/shard_map/all_to_all | solution.py:22
  719.4 5.4 copy-start.47
  (44 other events, 33.9 us)
where the time goes:
time: 836 us; the launch traced here: 826 us
  blocking collectives  547 us (65%)
  local copies, waits for them, and re-layouts  88.4 us (11%)
  waiting for transfers between devices  64.6 us (8%)
  other arithmetic  55.6 us (7%)
  starting transfers between devices  50.1 us (6%)
  matrix products  17.5 us (2%)
    psum x24, blocking collectives, over_axes(): value = lax.psum(value, axis)  276 us
    all_to_all x9, blocking collectives, copy_for_each(): lax.all_to_all(jnp.broadcast_to(value[None], (peers, *value.shape)), axis...  271 us
    all_to_all x3, waiting for transfers between devices, copy_for_each(): lax.all_to_all(jnp.broadcast_to(value[None], (peers, *value.shape)), axis...  63.8 us
    another operation x4, other arithmetic, body(): factor = jnp.linalg.cholesky(gram)  29.5 us
    unnamed x139, local copies, waits for them, and re-layouts  26.8 us
    all_to_all x3, starting transfers between devices, copy_for_each(): lax.all_to_all(jnp.broadcast_to(value[None], (peers, *value.shape)), axis...  25.7 us
    ppermute x12, starting transfers between devices, passed_along(): return lax.ppermute(block, axis, route)  24.4 us
    slice x6, local copies, waits for them, and re-layouts, coupling_rows(): even_rows = gathered[:, 0::2]  19.9 us
  transfers between devices with their start and end apart: 15, of which 6 were waited for; matrix products, arithmetic and copies ran while one was open for 3% of the time, Pallas kernels for 0%

commit v1 on v0

--- a/solution.py
+++ b/solution.py
@@ -37,7 +37,7 @@
 
 def over_axes(value, axes):
     for axis in axes:
-        value = lax.psum(value, axis)
+        value = jnp.sum(lax.all_gather(value, axis), axis=0)
     return value
 
 

time: 836 us -> 894 us (1.069)
  the two profiles are of different devices: /device:TPU:2 before, /device:TPU:8 now
where the time goes in v1:
time: 894 us; the launch traced here: 883 us
  blocking collectives  599 us (67%)
  local copies, waits for them, and re-layouts  94.7 us (11%)
  waiting for transfers between devices  64.4 us (7%)
  other arithmetic  56.1 us (6%)
  starting transfers between devices  45.7 us (5%)
  matrix products  17.5 us (2%)
    all_to_all x9, blocking collectives, copy_for_each(): lax.all_to_all(jnp.broadcast_to(value[None], (peers, *value.shape)), axis...  276 us
    all_gather x20, blocking collectives, over_axes(): value = jnp.sum(lax.all_gather(value, axis), axis=0)  272 us
    all_to_all x3, waiting for transfers between devices, copy_for_each(): lax.all_to_all(jnp.broadcast_to(value[None], (peers, *value.shape)), axis...  63.6 us
    unnamed x4, blocking collectives  51.8 us
    unnamed x150, local copies, waits for them, and re-layouts  32.7 us
    another operation x4, other arithmetic, body(): factor = jnp.linalg.cholesky(gram)  29.5 us
    ppermute x12, starting transfers between devices, passed_along(): return lax.ppermute(block, axis, route)  24.5 us
    all_to_all x3, starting transfers between devices, copy_for_each(): lax.all_to_all(jnp.broadcast_to(value[None], (peers, *value.shape)), axis...  21.2 us
  transfers between devices with their start and end apart: 15, of which 6 were waited for; matrix products, arithmetic and copies ran while one was open for 3% of the time, Pallas kernels for 0%

profile of v1, /device:TPU:8, one launch (start us, length us, event | category | flops | bytes accessed | tf_op | source)
XLA Modules:
  0.0 882.8 jit_solution(3531138959713462353)
XLA Ops:
  2.9 10.2 %all-to-all-start = ((bf16[32,2,64,128]{3,2,1,0:T(8,128)(2,1)}), bf16[32,2,64,128]{3,2,1,0:T(8,128)(2,1)S(1)}, u32[]{:S(2)}, u32[]{:S(2)}) async-start(bf16[32,2,64,128]{3,2,1,0:T(8,128)(2,1)} %broadcast_in_dim.37), calls=%async_computation | async-start | bytes 2097152 | tf_op jit(solution)/shard_map/all_to_all | solution.py:22
  19.1 22.5 %all-to-all-done = bf16[32,2,64,128]{3,2,1,0:T(8,128)(2,1)S(1)} async-done(((bf16[32,2,64,128]{3,2,1,0:T(8,128)(2,1)}), bf16[32,2,64,128]{3,2,1,0:T(8,128)(2,1)S(1)}, u32[]{:S(2)}, u32[]{:S(2)}) %all-to-all-start) | async-done | bytes 1048608 | tf_op jit(solution)/shard_map/all_to_all | solution.py:22
  69.5 19.3 %all-to-all-done.1 = bf16[32,2,64,128]{3,2,1,0:T(8,128)(2,1)S(1)} async-done(((bf16[32,2,64,128]{3,2,1,0:T(8,128)(2,1)}), bf16[32,2,64,128]{3,2,1,0:T(8,128)(2,1)S(1)}, u32[]{:S(2)}, u32[]{:S(2)}) %all-to-all-start.1) | async-done | bytes 1048608 | tf_op jit(solution)/shard_map/all_to_all | solution.py:22
  90.9 26.4 %all-reduce = f32[512]{0:T(512)S(1)} all-reduce(f32[512]{0:T(512)S(1)} %add_dynamic-update-slice_fusion), channel_id=2, replica_groups=mesh['sub_0'=8,'sub_1'=2,'blk_0'=4,'blk_1'=8] {'sub_0'}, use_global_device_ids=true, to_apply=%add | all-reduce | flops 512 | bytes 4096
  120.4 8.9 %all-reduce.2 = f32[256]{0:T(256)S(1)} all-reduce(f32[256]{0:T(256)S(1)} %dynamic-update-slice.5), channel_id=4, replica_groups=mesh['sub_0'=8,'sub_1'=2,'blk_0'=4,'blk_1'=8] {'blk_0'}, use_global_device_ids=true, to_apply=%add.2 | all-reduce | flops 256 | bytes 2048
  129.6 14.1 %all-reduce.3 = f32[512]{0:T(512)S(1)} all-reduce(f32[512]{0:T(512)S(1)} %dynamic-update-slice.6), channel_id=5, replica_groups=mesh['sub_0'=8,'sub_1'=2,'blk_0'=4,'blk_1'=8] {'blk_1'}, use_global_device_ids=true, to_apply=%add.3 | all-reduce | flops 512 | bytes 4096
  144.8 30.0 %all_to_all.60 = bf16[32,2,64,128]{3,2,1,0:T(8,128)(2,1)S(1)} all-to-all(bf16[32,2,64,128]{3,2,1,0:T(8,128)(2,1)S(1)} %broadcast_in_dim.39), channel_id=1, replica_groups=mesh['sub_0'=8,'sub_1'=2,'blk_0'=4,'blk_1'=8] {'blk_0','blk_1'}, dimensions={0} | all-to-all | bytes 2097152 | tf_op jit(solution)/shard_map/all_to_all | solution.py:22
  192.3 33.6 %all_to_all.65 = bf16[32,2,64,128]{3,2,1,0:T(8,128)(2,1)S(1)} all-to-all(bf16[32,2,64,128]{3,2,1,0:T(8,128)(2,1)S(1)} %broadcast_in_dim.40), channel_id=1, replica_groups=mesh['sub_0'=8,'sub_1'=2,'blk_0'=4,'blk_1'=8] {'blk_0','blk_1'}, dimensions={0} | all-to-all | bytes 2097152 | tf_op jit(solution)/shard_map/all_to_all | solution.py:22
  227.9 14.2 %all-gather.24 = f32[8,2,64]{2,1,0:T(2,128)S(1)} all-gather(f32[1,2,64]{2,1,0:T(2,128)S(1)} %maximum_bitcast_fusion.4), channel_id=6, replica_groups=mesh['sub_0'=8,'sub_1'=2,'blk_0'=4,'blk_1'=8] {'sub_0'}, dimensions={0}, use_global_device_ids=true | all-gather | bytes 4608 | tf_op jit(solution)/shard_map/all_gather | solution.py:40
  244.0 8.2 all-gather.26
  252.1 13.1 %all-gather.27 = f32[8,2,64]{2,1,0:T(2,128)S(1)} all-gather(f32[1,2,64]{2,1,0:T(2,128)S(1)} %bitcast.827), channel_id=9, replica_groups=mesh['sub_0'=8,'sub_1'=2,'blk_0'=4,'blk_1'=8] {'blk_1'}, dimensions={0}, use_global_device_ids=true | all-gather | bytes 4608 | tf_op jit(solution)/shard_map/all_gather | solution.py:40
  266.7 30.3 %all_to_all.61 = bf16[32,2,64,128]{3,2,1,0:T(8,128)(2,1)S(1)} all-to-all(bf16[32,2,64,128]{3,2,1,0:T(8,128)(2,1)S(1)} %broadcast_in_dim.41), channel_id=1, replica_groups=mesh['sub_0'=8,'sub_1'=2,'blk_0'=4,'blk_1'=8] {'blk_0','blk_1'}, dimensions={0} | all-to-all | bytes 2097152 | tf_op jit(solution)/shard_map/all_to_all | solution.py:22
  316.6 34.7 %all_to_all.66 = bf16[32,2,64,128]{3,2,1,0:T(8,128)(2,1)S(1)} all-to-all(bf16[32,2,64,128]{3,2,1,0:T(8,128)(2,1)S(1)} %broadcast_in_dim.42), channel_id=1, replica_groups=mesh['sub_0'=8,'sub_1'=2,'blk_0'=4,'blk_1'=8] {'blk_0','blk_1'}, dimensions={0} | all-to-all | bytes 2097152 | tf_op jit(solution)/shard_map/all_to_all | solution.py:22
  353.4 22.4 %all-gather.28 = f32[8,3,64]{2,1,0:T(4,128)S(1)} all-gather(f32[1,3,64]{2,1,0:T(4,128)S(1)} %maximum_bitcast_fusion.2), channel_id=10, replica_groups=mesh['sub_0'=8,'sub_1'=2,'blk_0'=4,'blk_1'=8] {'sub_0'}, dimensions={0}, use_global_device_ids=true | all-gather | bytes 6912 | tf_op jit(solution)/shard_map/all_gather | solution.py:40
  377.6 10.4 %all-gather.30 = f32[4,3,64]{2,1,0:T(4,128)S(1)} all-gather(f32[1,3,64]{2,1,0:T(4,128)S(1)} %bitcast.821), channel_id=12, replica_groups=mesh['sub_0'=8,'sub_1'=2,'blk_0'=4,'blk_1'=8] {'blk_0'}, dimensions={0}, use_global_device_ids=true | all-gather | bytes 3840 | tf_op jit(solution)/shard_map/all_gather | solution.py:40
  388.1 21.0 %all-gather.31 = f32[8,3,64]{2,1,0:T(4,128)S(1)} all-gather(f32[1,3,64]{2,1,0:T(4,128)S(1)} %bitcast.823), channel_id=13, replica_groups=mesh['sub_0'=8,'sub_1'=2,'blk_0'=4,'blk_1'=8] {'blk_1'}, dimensions={0}, use_global_device_ids=true | all-gather | bytes 6912 | tf_op jit(solution)/shard_map/all_gather | solution.py:40
  410.7 26.7 %all_to_all.62 = bf16[32,2,64,128]{3,2,1,0:T(8,128)(2,1)S(1)} all-to-all(bf16[32,2,64,128]{3,2,1,0:T(8,128)(2,1)S(1)} %broadcast_in_dim.43), channel_id=1, replica_groups=mesh['sub_0'=8,'sub_1'=2,'blk_0'=4,'blk_1'=8] {'blk_0','blk_1'}, dimensions={0} | all-to-all | bytes 2097152 | tf_op jit(solution)/shard_map/all_to_all | solution.py:22
  458.4 33.9 %all_to_all.67 = bf16[32,2,64,128]{3,2,1,0:T(8,128)(2,1)S(1)} all-to-all(bf16[32,2,64,128]{3,2,1,0:T(8,128)(2,1)S(1)} %broadcast_in_dim.44), channel_id=1, replica_groups=mesh['sub_0'=8,'sub_1'=2,'blk_0'=4,'blk_1'=8] {'blk_0','blk_1'}, dimensions={0} | all-to-all | bytes 2097152 | tf_op jit(solution)/shard_map/all_to_all | solution.py:22
  494.5 21.3 %all-gather.32 = f32[8,4,64]{2,1,0:T(4,128)S(1)} all-gather(f32[1,4,64]{2,1,0:T(4,128)S(1)} %maximum_bitcast_fusion.3), channel_id=14, replica_groups=mesh['sub_0'=8,'sub_1'=2,'blk_0'=4,'blk_1'=8] {'sub_0'}, dimensions={0}, use_global_device_ids=true | all-gather | bytes 9216 | tf_op jit(solution)/shard_map/all_gather | solution.py:40
  517.7 10.4 %all-gather.34 = f32[4,4,64]{2,1,0:T(4,128)S(1)} all-gather(f32[1,4,64]{2,1,0:T(4,128)S(1)} %bitcast.822), channel_id=16, replica_groups=mesh['sub_0'=8,'sub_1'=2,'blk_0'=4,'blk_1'=8] {'blk_0'}, dimensions={0}, use_global_device_ids=true | all-gather | bytes 5120 | tf_op jit(solution)/shard_map/all_gather | solution.py:40
  528.2 21.0 %all-gather.35 = f32[8,4,64]{2,1,0:T(4,128)S(1)} all-gather(f32[1,4,64]{2,1,0:T(4,128)S(1)} %bitcast.824), channel_id=17, replica_groups=mesh['sub_0'=8,'sub_1'=2,'blk_0'=4,'blk_1'=8] {'blk_1'}, dimensions={0}, use_global_device_ids=true | all-gather | bytes 9216 | tf_op jit(solution)/shard_map/all_gather | solution.py:40
  550.7 26.8 %all_to_all.63 = bf16[32,2,64,128]{3,2,1,0:T(8,128)(2,1)S(1)} all-to-all(bf16[32,2,64,128]{3,2,1,0:T(8,128)(2,1)S(1)} %broadcast_in_dim.45), channel_id=1, replica_groups=mesh['sub_0'=8,'sub_1'=2,'blk_0'=4,'blk_1'=8] {'blk_0','blk_1'}, dimensions={0} | all-to-all | bytes 2097152 | tf_op jit(solution)/shard_map/all_to_all | solution.py:22
  599.7 34.7 %all_to_all.68 = bf16[32,2,64,128]{3,2,1,0:T(8,128)(2,1)S(1)} all-to-all(bf16[32,2,64,128]{3,2,1,0:T(8,128)(2,1)S(1)} %broadcast_in_dim.46), channel_id=1, replica_groups=mesh['sub_0'=8,'sub_1'=2,'blk_0'=4,'blk_1'=8] {'blk_0','blk_1'}, dimensions={0} | all-to-all | bytes 2097152 | tf_op jit(solution)/shard_map/all_to_all | solution.py:22
  636.7 24.7 %all-gather.36 = f32[8,5,64]{2,1,0:T(8,128)S(1)} all-gather(f32[1,5,64]{2,1,0:T(8,128)S(1)} %bitcast.815), channel_id=18, replica_groups=mesh['sub_0'=8,'sub_1'=2,'blk_0'=4,'blk_1'=8] {'sub_0'}, dimensions={0}, use_global_device_ids=true | all-gather | bytes 11520 | tf_op jit(solution)/shard_map/all_gather | solution.py:40
  663.2 12.0 %all-gather.38 = f32[4,5,64]{2,1,0:T(8,128)S(1)} all-gather(f32[1,5,64]{2,1,0:T(8,128)S(1)} %bitcast.811), channel_id=20, replica_groups=mesh['sub_0'=8,'sub_1'=2,'blk_0'=4,'blk_1'=8] {'blk_0'}, dimensions={0}, use_global_device_ids=true | all-gather | bytes 6400 | tf_op jit(solution)/shard_map/all_gather | solution.py:40
  675.2 23.5 %all-gather.39 = f32[8,5,64]{2,1,0:T(8,128)S(1)} all-gather(f32[1,5,64]{2,1,0:T(8,128)S(1)} %bitcast.817), channel_id=21, replica_groups=mesh['sub_0'=8,'sub_1'=2,'blk_0'=4,'blk_1'=8] {'blk_1'}, dimensions={0}, use_global_device_ids=true | all-gather | bytes 11520 | tf_op jit(solution)/shard_map/all_gather | solution.py:40
  700.9 25.4 %all_to_all.64 = bf16[32,2,64,128]{3,2,1,0:T(8,128)(2,1)S(1)} all-to-all(bf16[32,2,64,128]{3,2,1,0:T(8,128)(2,1)S(1)} %broadcast_in_dim.47), channel_id=1, replica_groups=mesh['sub_0'=8,'sub_1'=2,'blk_0'=4,'blk_1'=8] {'blk_0','blk_1'}, dimensions={0} | all-to-all | bytes 2097152 | tf_op jit(solution)/shard_map/all_to_all | solution.py:22
  762.3 21.8 %all-to-all-done.11 = bf16[32,2,64,128]{3,2,1,0:T(8,128)(2,1)S(1)} async-done(((bf16[32,2,64,128]{3,2,1,0:T(8,128)(2,1)}), bf16[32,2,64,128]{3,2,1,0:T(8,128)(2,1)S(1)}, u32[]{:S(2)}, u32[]{:S(2)}) %all-to-all-start.11) | async-done | bytes 1048608 | tf_op jit(solution)/shard_map/all_to_all | solution.py:22
  787.2 24.7 %all-gather.40 = f32[8,6,64]{2,1,0:T(8,128)S(1)} all-gather(f32[1,6,64]{2,1,0:T(8,128)S(1)} %bitcast.814), channel_id=22, replica_groups=mesh['sub_0'=8,'sub_1'=2,'blk_0'=4,'blk_1'=8] {'sub_0'}, dimensions={0}, use_global_device_ids=true | all-gather | bytes 13824 | tf_op jit(solution)/shard_map/all_gather | solution.py:40
  813.7 12.0 %all-gather.42 = f32[4,6,64]{2,1,0:T(8,128)S(1)} all-gather(f32[1,6,64]{2,1,0:T(8,128)S(1)} %bitcast.813), channel_id=24, replica_groups=mesh['sub_0'=8,'sub_1'=2,'blk_0'=4,'blk_1'=8] {'blk_0'}, dimensions={0}, use_global_device_ids=true | all-gather | bytes 7680 | tf_op jit(solution)/shard_map/all_gather | solution.py:40
  825.7 23.5 %all-gather.43 = f32[8,6,64]{2,1,0:T(8,128)S(1)} all-gather(f32[1,6,64]{2,1,0:T(8,128)S(1)} %bitcast.818), channel_id=25, replica_groups=mesh['sub_0'=8,'sub_1'=2,'blk_0'=4,'blk_1'=8] {'blk_1'}, dimensions={0}, use_global_device_ids=true | all-gather | bytes 13824 | tf_op jit(solution)/shard_map/all_gather | solution.py:40
  851.2 29.4 %custom-call.11 = f32[64,5,5]{2,1,0:T(8,128)S(1)} custom-call(f32[64,5,5]{2,1,0:T(8,128)S(1)} %fusion), custom_call_target="Cholesky" | custom-call | tf_op jit(solution)/shard_map/jit(cholesky)/cholesky | solution.py:147
  (536 shorter events, 186.8 us)
Async XLA Ops:
  0.0 52.3 %copy-start = (bf16[1,2,64,2048]{3,2,1,0:T(8,128)(2,1)S(1)}, bf16[1,2,64,2048]{3,2,1,0:T(8,128)(2,1)}, u32[]{:S(2)}) copy-start(bf16[1,2,64,2048]{3,2,1,0:T(8,128)(2,1)} %param.16) | copy-start | bytes 1572868
  2.9 38.7 %all-to-all-start = ((bf16[32,2,64,128]{3,2,1,0:T(8,128)(2,1)}), bf16[32,2,64,128]{3,2,1,0:T(8,128)(2,1)S(1)}, u32[]{:S(2)}, u32[]{:S(2)}) async-start(bf16[32,2,64,128]{3,2,1,0:T(8,128)(2,1)} %broadcast_in_dim.37), calls=%async_computation | async-start | bytes 2097152 | tf_op jit(solution)/shard_map/all_to_all | solution.py:22
  18.3 167.1 %copy-start.30 = (pred[32]{0:T(512)(128)(4,1)}, pred[32]{0:T(512)(128)(4,1)S(1)}, u32[]{:S(2)}) copy-start(pred[32]{0:T(512)(128)(4,1)S(1)} %get-tuple-element.40) | copy-start | bytes 100
  19.1 168.9 %copy-start.25 = (pred[32]{0:T(512)(128)(4,1)}, pred[32]{0:T(512)(128)(4,1)S(1)}, u32[]{:S(2)}) copy-start(pred[32]{0:T(512)(128)(4,1)S(1)} %get-tuple-element.38) | copy-start | bytes 100
  19.1 165.7 %copy-start.39 = (s32[1024]{0:T(1024)}, s32[1024]{0:T(1024)S(1)}, u32[]{:S(2)}) copy-start(s32[1024]{0:T(1024)S(1)} %get-tuple-element.215) | copy-start | bytes 12292
  19.1 168.2 %copy-start.38 = (s32[1024]{0:T(1024)}, s32[1024]{0:T(1024)S(1)}, u32[]{:S(2)}) copy-start(s32[1024]{0:T(1024)S(1)} %get-tuple-element.216) | copy-start | bytes 12292
  46.1 8.0 collective-permute-start
  48.6 5.7 collective-permute-start.1
  56.4 5.3 copy-start.24
  56.4 32.4 %all-to-all-start.1 = ((bf16[32,2,64,128]{3,2,1,0:T(8,128)(2,1)}), bf16[32,2,64,128]{3,2,1,0:T(8,128)(2,1)S(1)}, u32[]{:S(2)}, u32[]{:S(2)}) async-start(bf16[32,2,64,128]{3,2,1,0:T(8,128)(2,1)} %broadcast_in_dim.38), calls=%async_computation.1 | async-start | bytes 2097152 | tf_op jit(solution)/shard_map/all_to_all | solution.py:22
  184.2 2.6 copy-start.5
  185.5 6.2 collective-permute-start.3
  188.1 3.9 collective-permute-start.2
  306.4 3.9 copy-start.6
  309.0 6.3 collective-permute-start.5
  311.7 3.9 collective-permute-start.4
  447.3 3.9 copy-start.7
  450.0 6.6 collective-permute-start.7
  451.3 1.4 copy-start.27
  451.8 4.2 copy-start.17
  452.8 4.5 collective-permute-start.6
  588.1 3.9 copy-start.8
  590.7 7.2 collective-permute-start.9
  592.0 1.4 copy-start.28
  592.6 4.0 copy-start.18
  593.6 5.1 collective-permute-start.8
  736.9 4.1 copy-start.4
  739.5 7.4 collective-permute-start.11
  741.6 4.0 copy-start.16
  742.6 5.1 collective-permute-start.10
  749.7 34.4 %all-to-all-start.11 = ((bf16[32,2,64,128]{3,2,1,0:T(8,128)(2,1)}), bf16[32,2,64,128]{3,2,1,0:T(8,128)(2,1)S(1)}, u32[]{:S(2)}, u32[]{:S(2)}) async-start(bf16[32,2,64,128]{3,2,1,0:T(8,128)(2,1)} %broadcast_in_dim.48), calls=%async_computation.11 | async-start | bytes 2097152 | tf_op jit(solution)/shard_map/all_to_all | solution.py:22
  756.2 5.4 copy-start.47
  (44 other events, 33.9 us)
